TPU v7x, 32 devices: a whole 2x2x4 slice. The times are simulated.
32 devices in a mesh: dp: 16 (over z, y, core), chan: 2 (over x).
Axes of the slice: x: 2, y: 2, z: 4, core: 2. Of those that a mesh axis runs over, the one named last changes fastest.
Arguments:
- inputs: bfloat16 [768, 196, 1024], P('dp', None, 'chan'), may hold values from -6 to 6
- norm_gain: float32 [1024], P('chan'), may hold values from 0.5 to 1.5
- norm_bias: float32 [1024], P('chan'), may hold values from -3 to 3
- w_first: bfloat16 [512, 196], replicated, may hold values from -0.4375 to 0.4375
- b_first: float32 [512], replicated, may hold values from -3 to 3
- w_second: bfloat16 [196, 512], replicated, may hold values from -0.25 to 0.25
- upstream: bfloat16 [768, 196, 1024], P('dp', None, 'chan'), may hold values from -6 to 6
Outputs:
- grad_input: bfloat16 [768, 196, 1024], P('dp', None, 'chan')
- grad_first: float32 [512, 196], P('dp')
- grad_second: float32 [196, 512], P(None, 'dp')
- grad_bias_first: float32 [512], P('dp')
- grad_gain: float32 [1024], P('chan')
- grad_shift: float32 [1024], P('chan')
All inputs are finite; a program needn't handle non-finite values.
Results may differ from a plain program's by a relative error of at most 0.0056.
Values sent between devices are 32-bit elements; how exact they have to be, the bound alone decides.
No kernel may reach another device: no remote copies, remote signals or barrier semaphores. Data moves between devices by JAX's collectives and lax.ppermute only.
A program may use at most 192 MiB of HBM per device.

v0:
```python
import functools

import jax
import jax.numpy as jnp
from jax import lax
from jax.experimental import pallas as pl
from jax.experimental.pallas import tpu as pltpu
from jax.sharding import PartitionSpec as P

epsilon = 1e-06
f32 = jnp.float32
bf16 = jnp.bfloat16
NT = (((1,), (1,)), ((), ()))
NN = (((1,), (0,)), ((), ()))


def round_up(n, m):
    return -(-n // m) * m


def divisor(n, most):
    return max(d for d in range(1, most + 1) if n % d == 0)


def column(ref, b, lanes):
    return pltpu.roll(ref[...], lax.rem(lanes - b, lanes), 1)[:, 0:1]


def stats_kernel(x_ref, out_ref, *, step_images, half):
    step = pl.program_id(0)
    patches, width = x_ref.shape[1:]

    @pl.when(step == 0)
    def _():
        out_ref[...] = jnp.zeros_like(out_ref)

    lane = lax.broadcasted_iota(jnp.int32, (patches, out_ref.shape[1]), 1)
    acc = out_ref[0:patches, :]
    for j in range(step_images):
        b = step * step_images + j
        x = x_ref[j].astype(f32)
        total = jnp.sum(x, axis=1, keepdims=True)
        d = x - total * (1.0 / width)
        spread = jnp.sum(d * d, axis=1, keepdims=True)
        acc = jnp.where(lane == b, total, acc)
        acc = jnp.where(lane == half + b, spread, acc)
    out_ref[0:patches, :] = acc


def main_kernel(*refs, step_images, half, chans, chunk):
    stat_refs = refs[:chans]
    (x_ref, up_ref, gain_ref, bias_ref, w1_ref, w2t_ref, w1t_ref,
     u_ref, sums_ref, mean_ref, rstd_ref, grads_ref, params_ref) = refs[chans:chans + 13]
    mixed_ref, upper_ref, gp_ref = refs[chans + 13:]
    step = pl.program_id(0)
    patches, width = x_ref.shape[1:]
    hidden, depth = w1_ref.shape
    lanes = sums_ref.shape[1]

    @pl.when(step == 0)
    def _():
        row = lax.broadcasted_iota(jnp.int32, mixed_ref.shape[1:], 0)
        ones = jnp.where((row >= patches) & (row < patches + 3), 1.0, 0.0).astype(bf16)
        for j in range(step_images):
            mixed_ref[j] = ones
            upper_ref[j] = jnp.zeros(upper_ref.shape[1:], bf16)
        stats = [r[...] for r in stat_refs]
        full = width * chans
        mean = sum(stats) * (1.0 / full)
        spread = sum(stats)
        spread = pltpu.roll(spread, half, 1)
        for s in stats:
            off = s * (1.0 / width) - mean
            spread = spread + width * (off * off)
        mean_ref[...] = mean
        rstd_ref[...] = lax.rsqrt(spread * (1.0 / full) + epsilon)
        sums_ref[...] = jnp.zeros_like(sums_ref)
        grads_ref[...] = jnp.zeros_like(grads_ref)
        params_ref[...] = jnp.zeros_like(params_ref)

    gain = gain_ref[...]
    bias = bias_ref[...]
    lane = lax.broadcasted_iota(jnp.int32, (patches, lanes), 1)
    sums = sums_ref[0:patches, :]
    for j in range(step_images):
        b = step * step_images + j
        mean = column(mean_ref, b, lanes)[0:patches]
        rstd = column(rstd_ref, b, lanes)[0:patches]
        normed = (x_ref[j].astype(f32) - mean) * rstd
        mixed_ref[j, 0:patches, :] = (normed * gain + bias).astype(bf16)
        upper_ref[j, 0:patches, :] = up_ref[j]
        for k in range(0, hidden, chunk):
            ks = pl.ds(k, chunk)
            pre = lax.dot_general(w1_ref[ks, :], mixed_ref[j], NN, preferred_element_type=f32)
            act = lax.dot_general(w2t_ref[ks, :], upper_ref[j], NN, preferred_element_type=f32)
            cdf = 0.5 + 0.5 * lax.erf(pre * 0.7071067811865476)
            pdf = jnp.exp2((pre * pre) * -0.7213475204444817) * 0.3989422804014327
            activated = (pre * cdf).astype(bf16)
            gp = (act * (cdf + pre * pdf)).astype(bf16)
            gp_ref[j, ks, :] = gp
            grads_ref[ks, 0:depth] += lax.dot_general(gp, mixed_ref[j], NT, preferred_element_type=f32)
            grads_ref[ks, depth:] += lax.dot_general(
                activated, upper_ref[j], NT, preferred_element_type=f32
            )
        gm = lax.dot_general(w1t_ref[...], gp_ref[j], NN, preferred_element_type=f32)[0:patches]
        gmn = gm * normed
        params_ref[0:1, :] += jnp.sum(gmn, axis=0, keepdims=True)
        params_ref[1:2, :] += jnp.sum(gm, axis=0, keepdims=True)
        gn = gm * gain
        first = jnp.sum(gn, axis=1, keepdims=True)
        second = jnp.sum(gmn * gain, axis=1, keepdims=True)
        sums = jnp.where(lane == b, first, sums)
        sums = jnp.where(lane == half + b, second, sums)
        u_ref[j] = (up_ref[j].astype(f32) + rstd * gn).astype(bf16)
    sums_ref[0:patches, :] = sums


def finish_kernel(*refs, step_images, half, chans, start):
    sum_refs = refs[:chans]
    mean_ref, rstd_ref, x_ref, u_ref, out_ref, add_ref, mul_ref = refs[chans:]
    step = pl.program_id(0)
    patches, width = x_ref.shape[1:]
    lanes = mean_ref.shape[1]

    @pl.when(step == 0)
    def _():
        first = sum(r[...] for r in sum_refs) * (1.0 / (width * chans))
        second = pltpu.roll(first, half, 1)
        rstd = rstd_ref[...]
        slope = rstd * rstd * second
        mul_ref[...] = -slope
        add_ref[...] = mean_ref[...] * slope - rstd * first

    for j in range(step_images):
        b = start + step * step_images + j
        add = column(add_ref, b, lanes)[0:patches]
        mul = column(mul_ref, b, lanes)[0:patches]
        out_ref[j] = (u_ref[j].astype(f32) + (add + mul * x_ref[j].astype(f32))).astype(bf16)


def swap(value, axis, bit, size):
    return lax.ppermute(value, axis, [(i, i ^ bit) for i in range(size)])


def peers(value, axis, size):
    return [value] + [
        lax.ppermute(value, axis, [(i, (i + d) % size) for i in range(size)]) for d in range(1, size)
    ]


def whole(shape):
    return pl.BlockSpec(shape, lambda i: (0,) * len(shape))


def per_device(inputs, norm_gain, norm_bias, w_first, b_first, w_second, upstream):
    images, patches, width = inputs.shape
    hidden = w_first.shape[0]
    chans = lax.axis_size("chan")
    ranks = lax.axis_size("dp")
    scale = 1.0 / (images * ranks)
    lanes = round_up(2 * images, 128)
    half = lanes // 2
    rows = round_up(patches, 8)
    depth = round_up(patches + 3, 128)
    tall = round_up(patches, 16)
    stat_shape = (rows, lanes)
    stat_type = jax.ShapeDtypeStruct(stat_shape, f32)
    params = pltpu.CompilerParams(
        dimension_semantics=("arbitrary",), vmem_limit_bytes=56 * 1024 * 1024
    )

    def image_spec(n, base=0):
        return pl.BlockSpec((n, patches, width), lambda i: (base + i, 0, 0))

    n_a = divisor(images, 8)
    stats = pl.pallas_call(
        functools.partial(stats_kernel, step_images=n_a, half=half),
        grid=(images // n_a,),
        in_specs=[image_spec(n_a)],
        out_specs=whole(stat_shape),
        out_shape=stat_type,
        compiler_params=params,
        name="row_stats",
    )(inputs)
    stats = peers(stats, "chan", chans)

    top = lax.reduce_precision(b_first, 8, 7)
    rest = b_first - top
    mid = lax.reduce_precision(rest, 8, 7)
    low = rest - mid
    split = jnp.stack([top, mid, low], axis=1).astype(bf16)
    w1 = jnp.pad(jnp.concatenate([w_first, split], axis=1), ((0, 0), (0, depth - patches - 3)))
    w2t = jnp.pad(w_second.T, ((0, 0), (0, depth - patches)))
    w1t = jnp.pad(w_first.T, ((0, tall - patches), (0, 0)))

    n_b = divisor(images, 2)
    chunk = hidden // 2
    u, sums, mean, rstd, grads, norm_grads = pl.pallas_call(
        functools.partial(main_kernel, step_images=n_b, half=half, chans=chans, chunk=chunk),
        grid=(images // n_b,),
        in_specs=[whole(stat_shape)] * chans
        + [image_spec(n_b)] * 2
        + [whole((1, width))] * 2
        + [whole((hidden, depth))] * 2
        + [whole((tall, hidden))],
        out_specs=[
            image_spec(n_b),
            whole(stat_shape),
            whole(stat_shape),
            whole(stat_shape),
            whole((hidden, 2 * depth)),
            whole((8, width)),
        ],
        out_shape=[
            jax.ShapeDtypeStruct(inputs.shape, bf16),
            stat_type,
            stat_type,
            stat_type,
            jax.ShapeDtypeStruct((hidden, 2 * depth), f32),
            jax.ShapeDtypeStruct((8, width), f32),
        ],
        scratch_shapes=[
            pltpu.VMEM((n_b, depth, width), bf16),
            pltpu.VMEM((n_b, depth, width), bf16),
            pltpu.VMEM((n_b, hidden, width), bf16),
        ],
        compiler_params=params,
        name="mix_backward",
    )(*stats, inputs, upstream, norm_gain[None], norm_bias[None], w1, w2t, w1t)

    sums = peers(sums, "chan", chans)

    pieces = 4 if images % 4 == 0 else 1
    part = images // pieces
    n_c = divisor(part, 6)
    out = u
    for piece in range(pieces):
        base = piece * part // n_c
        out = pl.pallas_call(
            functools.partial(
                finish_kernel, step_images=n_c, half=half, chans=chans, start=piece * part
            ),
            grid=(part // n_c,),
            in_specs=[whole(stat_shape)] * (chans + 2) + [image_spec(n_c, base)] * 2,
            out_specs=image_spec(n_c, base),
            out_shape=jax.ShapeDtypeStruct(inputs.shape, bf16),
            scratch_shapes=[pltpu.VMEM(stat_shape, f32)] * 2,
            input_output_aliases={chans + 3: 0},
            compiler_params=params,
            cost_estimate=pl.CostEstimate(
                flops=part * patches * width * 60,
                bytes_accessed=part * patches * width * 6,
                transcendentals=0,
            ),
            name=f"finish_{piece}",
        )(*sums, mean, rstd, inputs, out)

    me = lax.axis_index("dp")
    if ranks & (ranks - 1) == 0:
        bits = ranks.bit_length() - 1
        part_grads = grads.reshape((ranks, hidden // ranks, 2 * depth))
        norm_grads = norm_grads[0:2]
        for bit in range(bits):
            mine = (me >> bit) & 1
            pairs = part_grads.reshape((-1, 2) + part_grads.shape[1:])
            give = lax.dynamic_index_in_dim(pairs, 1 - mine, 1, keepdims=False)
            keep = lax.dynamic_index_in_dim(pairs, mine, 1, keepdims=False)
            part_grads = keep + swap(give, "dp", 1 << bit, ranks)
            norm_grads = norm_grads + swap(norm_grads, "dp", 1 << bit, ranks)
        owned = part_grads[0]
    else:
        owned = lax.psum_scatter(grads, "dp", scatter_dimension=0, tiled=True)
        norm_grads = lax.psum(norm_grads, "dp")
    owned = sum(peers(owned, "chan", chans)) * scale
    norm_grads = norm_grads * scale
    return (
        out,
        owned[:, 0:patches],
        owned[:, depth:depth + patches].T,
        owned[:, patches],
        norm_grads[0],
        norm_grads[1],
    )


def solution(mesh):
    in_specs = (P("dp", None, "chan"), P("chan"), P("chan"), P(), P(), P(), P("dp", None, "chan"))
    out_specs = (P("dp", None, "chan"), P("dp", None), P(None, "dp"), P("dp"), P("chan"), P("chan"))
    return jax.shard_map(
        per_device, mesh=mesh, in_specs=in_specs, out_specs=out_specs, check_vma=False
    )
```

profile of v0, /device:TPU:0, one launch (start us, length us, event | category | flops | bytes accessed | tf_op | source)
XLA Modules:
  0.0 170.2 jit_solution(6444352636783170550)
XLA Ops:
  0.6 13.0 %copy.40.x_ref.refs_2_.refs_4_ = bf16[48,196,512]{2,1,0:T(8,128)(2,1)} copy(bf16[48,196,512]{2,0,1:T(8,128)(2,1)} %param.7) | data formatting | bytes 19267584 | tf_op args[0]
  13.6 9.2 %row_stats.1.refs_0_ = f32[200,128]{1,0:T(8,128)} custom-call(bf16[48,196,512]{2,1,0:T(8,128)(2,1)} %copy.40.x_ref.refs_2_.refs_4_), custom_call_target="tpu_custom_call" | custom-call | tf_op jit(solution)/shard_map/row_stats/pallas_call | solution.py:176
  22.8 3.0 %collective-permute-start = (f32[200,128]{1,0:T(8,128)}, f32[200,128]{1,0:T(8,128)S(1)}, u32[]{:S(2)}, u32[]{:S(2)}) collective-permute-start(f32[200,128]{1,0:T(8,128)} %row_stats.1.refs_0_), channel_id=1, source_target_pairs={{0,1},{1,0},{2,3},{3,2},{4,5},{5,4},{6,7},{7,6},{8,9},{9,8},{10,11... | collective-permute-start | bytes 307208 | tf_op jit(solution)/shard_map/ppermute | solution.py:147
  26.3 12.9 %copy.47.refs_3_ = bf16[48,196,512]{2,1,0:T(8,128)(2,1)} copy(bf16[48,196,512]{2,0,1:T(8,128)(2,1)} %param.13) | data formatting | bytes 19267584 | tf_op args[6]
  39.4 0.8 pad.13.refs_7_
  40.9 0.9 fusion.6.refs_6_
  42.4 62.4 %mix_backward.1 = (bf16[48,196,512]{2,1,0:T(8,128)(2,1)}, f32[200,128]{1,0:T(8,128)}, f32[200,128]{1,0:T(8,128)}, f32[200,128]{1,0:T(8,128)}, f32[512,512]{1,0:T(8,128)}, /*index=5*/f32[8,512]{1,0:T(8,128)}) custom-call(f32[200,128]{1,0:T(8,128)} %row_stats.1.refs_0_, f32[200,128]{1,0:T(8,128)} %copy-done.3, ...), custom_call_target="tpu_custom_call" | custom-call | tf_op jit(solution)/shard_map/mix_backward/pallas_call | solution.py:198
  104.9 1.1 dynamic-slice_bitcast_fusion
  106.0 1.9 %collective-permute-done.2 = f32[8,32,512]{2,1,0:T(8,128)S(1)} collective-permute-done((f32[8,32,512]{2,1,0:T(8,128)S(1)}, f32[8,32,512]{2,1,0:T(8,128)S(1)}, u32[]{:S(2)}, u32[]{:S(2)}) %collective-permute-start.2) | collective-permute-done | bytes 524320 | tf_op jit(solution)/shard_map/ppermute | solution.py:142
  107.9 1.1 bitcast_add_fusion
  109.1 1.6 collective-permute-start.3
  111.4 6.1 %collective-permute-done.3 = f32[4,32,512]{2,1,0:T(8,128)S(1)} collective-permute-done((f32[4,32,512]{2,1,0:T(8,128)S(1)}, f32[4,32,512]{2,1,0:T(8,128)S(1)}, u32[]{:S(2)}, u32[]{:S(2)}) %collective-permute-start.3) | collective-permute-done | bytes 262176 | tf_op jit(solution)/shard_map/ppermute | solution.py:142
  117.6 1.6 collective-permute-start.4
  119.9 1.5 collective-permute-start.8
  121.5 2.1 %collective-permute-done.8 = f32[2,512]{1,0:T(2,128)S(1)} collective-permute-done((f32[2,512]{1,0:T(2,128)S(1)}, f32[2,512]{1,0:T(2,128)S(1)}, u32[]{:S(2)}, u32[]{:S(2)}) %collective-permute-start.8) | collective-permute-done | bytes 4128 | tf_op jit(solution)/shard_map/ppermute | solution.py:142
  124.3 2.8 %collective-permute-done.9 = f32[2,512]{1,0:T(2,128)S(1)} collective-permute-done((f32[2,512]{1,0:T(2,128)S(1)}, f32[2,512]{1,0:T(2,128)S(1)}, u32[]{:S(2)}, u32[]{:S(2)}) %collective-permute-start.9) | collective-permute-done | bytes 4128 | tf_op jit(solution)/shard_map/ppermute | solution.py:142
  127.2 2.6 %collective-permute-start.10 = (f32[2,512]{1,0:T(2,128)S(1)}, f32[2,512]{1,0:T(2,128)S(1)}, u32[]{:S(2)}, u32[]{:S(2)}) collective-permute-start(f32[2,512]{1,0:T(2,128)S(1)} %add.80), channel_id=1, source_target_pairs={{0,16},{2,18},{4,20},{6,22},{8,24},{10,26},{12,28},{14,30},{16,0},... | collective-permute-start | bytes 12296 | tf_op jit(solution)/shard_map/ppermute | solution.py:142
  130.2 1.5 collective-permute-done.10
  131.7 3.9 %collective-permute-done.5 = f32[1,32,512]{2,1,0:T(8,128)S(1)} collective-permute-done((f32[1,32,512]{2,1,0:T(8,128)S(1)}, f32[1,32,512]{2,1,0:T(8,128)S(1)}, u32[]{:S(2)}, u32[]{:S(2)}) %collective-permute-start.5) | collective-permute-done | bytes 65568 | tf_op jit(solution)/shard_map/ppermute | solution.py:142
  137.5 5.1 %finish_0.1.refs_5_ = bf16[48,196,512]{2,1,0:T(8,128)(2,1)} custom-call(f32[200,128]{1,0:T(8,128)} %get-tuple-element.12.refs_0_, f32[200,128]{1,0:T(8,128)} %copy-done, f32[200,128]{1,0:T(8,128)} %get-tuple-element.13.refs_2_, f32[200,128]{1,0:T(8,128)} %get-tuple-element.14.refs_3_, ...), custom_call_target="tpu_custom_call", output_to_operand_aliasing={{}: (5, {})} | custom-call | flops 72253440 | bytes 7225344 | tf_op jit(solution)/shard_map/finish_0/pallas_call | solution.py:239
  142.6 5.1 %finish_1.1.refs_5_ = bf16[48,196,512]{2,1,0:T(8,128)(2,1)} custom-call(f32[200,128]{1,0:T(8,128)} %get-tuple-element.12.refs_0_, f32[200,128]{1,0:T(8,128)} %copy-done, f32[200,128]{1,0:T(8,128)} %get-tuple-element.13.refs_2_, f32[200,128]{1,0:T(8,128)} %get-tuple-element.14.refs_3_, ...), custom_call_target="tpu_custom_call", output_to_operand_aliasing={{}: (5, {})} | custom-call | flops 72253440 | bytes 7225344 | tf_op jit(solution)/shard_map/finish_1/pallas_call | solution.py:239
  147.7 5.1 %finish_2.1.refs_5_ = bf16[48,196,512]{2,1,0:T(8,128)(2,1)} custom-call(f32[200,128]{1,0:T(8,128)} %get-tuple-element.12.refs_0_, f32[200,128]{1,0:T(8,128)} %copy-done, f32[200,128]{1,0:T(8,128)} %get-tuple-element.13.refs_2_, f32[200,128]{1,0:T(8,128)} %get-tuple-element.14.refs_3_, ...), custom_call_target="tpu_custom_call", output_to_operand_aliasing={{}: (5, {})} | custom-call | flops 72253440 | bytes 7225344 | tf_op jit(solution)/shard_map/finish_2/pallas_call | solution.py:239
  152.8 5.1 %finish_3.1 = bf16[48,196,512]{2,1,0:T(8,128)(2,1)} custom-call(f32[200,128]{1,0:T(8,128)} %get-tuple-element.12.refs_0_, f32[200,128]{1,0:T(8,128)} %copy-done, f32[200,128]{1,0:T(8,128)} %get-tuple-element.13.refs_2_, f32[200,128]{1,0:T(8,128)} %get-tuple-element.14.refs_3_, ...), custom_call_target="tpu_custom_call", output_to_operand_aliasing={{}: (5, {})} | custom-call | flops 72253440 | bytes 7225344 | tf_op jit(solution)/shard_map/finish_3/pallas_call | solution.py:239
  157.9 11.0 %copy.52 = bf16[48,196,512]{2,0,1:T(8,128)(2,1)} copy(bf16[48,196,512]{2,1,0:T(8,128)(2,1)} %finish_3.1) | data formatting | bytes 19267584
  (43 shorter events, 8.0 us)
Async XLA Ops:
  13.6 12.2 %copy-start.4 = (f32[512]{0:T(512)S(1)}, f32[512]{0:T(512)}, u32[]{:S(2)}) copy-start(f32[512]{0:T(512)} %param.11) | copy-start | bytes 6148
  13.6 12.6 %copy-start.1 = (bf16[512,196]{0,1:T(8,128)(2,1)S(1)}, bf16[512,196]{0,1:T(8,128)(2,1)}, u32[]{:S(2)}) copy-start(bf16[512,196]{0,1:T(8,128)(2,1)} %param.10) | copy-start | bytes 602116
  22.8 19.0 %collective-permute-start = (f32[200,128]{1,0:T(8,128)}, f32[200,128]{1,0:T(8,128)S(1)}, u32[]{:S(2)}, u32[]{:S(2)}) collective-permute-start(f32[200,128]{1,0:T(8,128)} %row_stats.1.refs_0_), channel_id=1, source_target_pairs={{0,1},{1,0},{2,3},{3,2},{4,5},{5,4},{6,7},{7,6},{8,9},{9,8},{10,11... | collective-permute-start | bytes 307208 | tf_op jit(solution)/shard_map/ppermute | solution.py:147
  26.3 12.9 %copy-start.2 = (bf16[196,512]{1,0:T(8,128)(2,1)S(1)}, bf16[196,512]{1,0:T(8,128)(2,1)}, u32[]{:S(2)}) copy-start(bf16[196,512]{1,0:T(8,128)(2,1)} %param.12) | copy-start | bytes 602116
  41.8 0.6 copy-start.3
  106.0 2.0 %collective-permute-start.2 = (f32[8,32,512]{2,1,0:T(8,128)S(1)}, f32[8,32,512]{2,1,0:T(8,128)S(1)}, u32[]{:S(2)}, u32[]{:S(2)}) collective-permute-start(f32[8,32,512]{2,1,0:T(8,128)S(1)} %dynamic-slice_bitcast_fusion), channel_id=1, source_target_pairs={{0,2},{2,0},{4,6},{6,4},{8,10},{10,8},{12,14},{14,12},{16,18},{18,... | collective-permute-start | bytes 1572872 | tf_op jit(solution)/shard_map/ppermute | solution.py:142
  109.1 8.4 %collective-permute-start.3 = (f32[4,32,512]{2,1,0:T(8,128)S(1)}, f32[4,32,512]{2,1,0:T(8,128)S(1)}, u32[]{:S(2)}, u32[]{:S(2)}) collective-permute-start(f32[4,32,512]{2,1,0:T(8,128)S(1)} %dynamic-slice_bitcast_fusion.1), channel_id=1, source_target_pairs={{0,4},{2,6},{4,0},{6,2},{8,12},{10,14},{12,8},{14,10},{16,20},{18,... | collective-permute-start | bytes 786440 | tf_op jit(solution)/shard_map/ppermute | solution.py:142
  111.4 7.8 %collective-permute-start.7 = (f32[2,512]{1,0:T(2,128)S(1)}, f32[2,512]{1,0:T(2,128)S(1)}, u32[]{:S(2)}, u32[]{:S(2)}) collective-permute-start(f32[2,512]{1,0:T(2,128)S(1)} %slice.21), channel_id=1, source_target_pairs={{0,2},{2,0},{4,6},{6,4},{8,10},{10,8},{12,14},{14,12},{16,18},{18,... | collective-permute-start | bytes 12296 | tf_op jit(solution)/shard_map/ppermute | solution.py:142
  117.6 12.2 %collective-permute-start.4 = (f32[2,32,512]{2,1,0:T(8,128)S(1)}, f32[2,32,512]{2,1,0:T(8,128)S(1)}, u32[]{:S(2)}, u32[]{:S(2)}) collective-permute-start(f32[2,32,512]{2,1,0:T(8,128)S(1)} %dynamic-slice_bitcast_fusion.2), channel_id=1, source_target_pairs={{0,8},{2,10},{4,12},{6,14},{8,0},{10,2},{12,4},{14,6},{16,24},{18,... | collective-permute-start | bytes 393224 | tf_op jit(solution)/shard_map/ppermute | solution.py:142
  119.9 3.6 %collective-permute-start.8 = (f32[2,512]{1,0:T(2,128)S(1)}, f32[2,512]{1,0:T(2,128)S(1)}, u32[]{:S(2)}, u32[]{:S(2)}) collective-permute-start(f32[2,512]{1,0:T(2,128)S(1)} %slice_add_fusion), channel_id=1, source_target_pairs={{0,4},{2,6},{4,0},{6,2},{8,12},{10,14},{12,8},{14,10},{16,20},{18,... | collective-permute-start | bytes 12296 | tf_op jit(solution)/shard_map/ppermute | solution.py:142
  123.6 3.6 %collective-permute-start.9 = (f32[2,512]{1,0:T(2,128)S(1)}, f32[2,512]{1,0:T(2,128)S(1)}, u32[]{:S(2)}, u32[]{:S(2)}) collective-permute-start(f32[2,512]{1,0:T(2,128)S(1)} %add.79), channel_id=1, source_target_pairs={{0,8},{2,10},{4,12},{6,14},{8,0},{10,2},{12,4},{14,6},{16,24},{18,... | collective-permute-start | bytes 12296 | tf_op jit(solution)/shard_map/ppermute | solution.py:142
  124.0 12.8 %collective-permute-start.1 = (f32[200,128]{1,0:T(8,128)}, f32[200,128]{1,0:T(8,128)S(1)}, u32[]{:S(2)}, u32[]{:S(2)}) collective-permute-start(f32[200,128]{1,0:T(8,128)} %get-tuple-element.12.refs_0_), channel_id=1, source_target_pairs={{0,1},{1,0},{2,3},{3,2},{4,5},{5,4},{6,7},{7,6},{8,9},{9,8},{10,11... | collective-permute-start | bytes 307208 | tf_op jit(solution)/shard_map/ppermute | solution.py:147
  127.2 4.5 %collective-permute-start.10 = (f32[2,512]{1,0:T(2,128)S(1)}, f32[2,512]{1,0:T(2,128)S(1)}, u32[]{:S(2)}, u32[]{:S(2)}) collective-permute-start(f32[2,512]{1,0:T(2,128)S(1)} %add.80), channel_id=1, source_target_pairs={{0,16},{2,18},{4,20},{6,22},{8,24},{10,26},{12,28},{14,30},{16,0},... | collective-permute-start | bytes 12296 | tf_op jit(solution)/shard_map/ppermute | solution.py:142
  129.8 5.8 %collective-permute-start.5 = (f32[1,32,512]{2,1,0:T(8,128)S(1)}, f32[1,32,512]{2,1,0:T(8,128)S(1)}, u32[]{:S(2)}, u32[]{:S(2)}) collective-permute-start(f32[1,32,512]{2,1,0:T(8,128)S(1)} %constant_dynamic-slice_fusion), channel_id=1, source_target_pairs={{0,16},{2,18},{4,20},{6,22},{8,24},{10,26},{12,28},{14,30},{16,0},... | collective-permute-start | bytes 196616 | tf_op jit(solution)/shard_map/ppermute | solution.py:142
  135.6 33.2 %collective-permute-start.6 = (f32[32,512]{1,0:T(8,128)S(1)}, f32[32,512]{1,0:T(8,128)S(1)}, u32[]{:S(2)}, u32[]{:S(2)}) collective-permute-start(f32[32,512]{1,0:T(8,128)S(1)} %add_bitcast_fusion), channel_id=1, source_target_pairs={{0,1},{1,0},{2,3},{3,2},{4,5},{5,4},{6,7},{7,6},{8,9},{9,8},{10,11... | collective-permute-start | bytes 196616 | tf_op jit(solution)/shard_map/ppermute | solution.py:147
  136.8 0.6 copy-start
where the time goes:
time: 171 us; the launch traced here: 170 us
  Pallas kernels  92 us (54%)
  local copies, waits for them, and re-layouts  44 us (26%)
  waiting for transfers between devices  18.4 us (11%)
  starting transfers between devices  12.1 us (7%)
  other arithmetic  2.87 us (2%)
    pallas_call x1, Pallas kernels, per_device(): pl.pallas_call(functools.partial(main_kernel, step_images=n_b, half=half,...  62.4 us
    unnamed x15, local copies, waits for them, and re-layouts  38.4 us
    pallas_call x4, Pallas kernels, per_device(): pl.pallas_call(functools.partial(finish_kernel, step_images=n_c, half=hal...  20.4 us
    ppermute x8, waiting for transfers between devices, swap(): return lax.ppermute(value, axis, [(i, i ^ bit) for i in range(size)])  18.3 us
    pallas_call x1, Pallas kernels, per_device(): pl.pallas_call(functools.partial(stats_kernel, step_images=n_a, half=half...  9.21 us
    ppermute x8, starting transfers between devices, swap(): return lax.ppermute(value, axis, [(i, i ^ bit) for i in range(size)])  8.26 us
    ppermute x3, starting transfers between devices, peers(): lax.ppermute(value, axis, [(i, (i + d) % size) for i in range(size)])  3.88 us
  transfers between devices with their start and end apart: 11, of which 6 were waited for; matrix products, arithmetic and copies ran while one was open for 17% of the time, Pallas kernels for 12%

commit v1 on v0

--- a/solution.py
+++ b/solution.py
@@ -230,13 +230,17 @@
 
     sums = peers(sums, "chan", chans)
 
-    pieces = 4 if images % 4 == 0 else 1
+    held = lax.optimization_barrier((grads, norm_grads, *sums))
+    grads, norm_grads, sums = held[0], held[1][0:2], list(held[2:])
+    paired = ranks & (ranks - 1) == 0
+    bits = ranks.bit_length() - 1 if paired else 1
+    pieces = divisor(images, bits)
     part = images // pieces
     n_c = divisor(part, 6)
-    out = u
-    for piece in range(pieces):
+
+    def finish(piece, out):
         base = piece * part // n_c
-        out = pl.pallas_call(
+        return pl.pallas_call(
             functools.partial(
                 finish_kernel, step_images=n_c, half=half, chans=chans, start=piece * part
             ),
@@ -248,7 +252,7 @@
             input_output_aliases={chans + 3: 0},
             compiler_params=params,
             cost_estimate=pl.CostEstimate(
-                flops=part * patches * width * 60,
+                flops=part * patches * width * 200,
                 bytes_accessed=part * patches * width * 6,
                 transcendentals=0,
             ),
@@ -256,19 +260,24 @@
         )(*sums, mean, rstd, inputs, out)
 
     me = lax.axis_index("dp")
-    if ranks & (ranks - 1) == 0:
-        bits = ranks.bit_length() - 1
+    out = u
+    if paired:
         part_grads = grads.reshape((ranks, hidden // ranks, 2 * depth))
-        norm_grads = norm_grads[0:2]
-        for bit in range(bits):
-            mine = (me >> bit) & 1
+        for r in range(bits):
+            mine = (me >> r) & 1
             pairs = part_grads.reshape((-1, 2) + part_grads.shape[1:])
             give = lax.dynamic_index_in_dim(pairs, 1 - mine, 1, keepdims=False)
             keep = lax.dynamic_index_in_dim(pairs, mine, 1, keepdims=False)
-            part_grads = keep + swap(give, "dp", 1 << bit, ranks)
-            norm_grads = norm_grads + swap(norm_grads, "dp", 1 << bit, ranks)
+            give = swap(give, "dp", 1 << r, ranks)
+            other = swap(norm_grads, "dp", 1 << r, ranks)
+            if r < pieces:
+                out = finish(r, out)
+                give, other, out = lax.optimization_barrier((give, other, out))
+            part_grads = keep + give
+            norm_grads = norm_grads + other
         owned = part_grads[0]
     else:
+        out = finish(0, out)
         owned = lax.psum_scatter(grads, "dp", scatter_dimension=0, tiled=True)
         norm_grads = lax.psum(norm_grads, "dp")
     owned = sum(peers(owned, "chan", chans)) * scale

time: 171 us -> 155 us (0.906)
  waiting for transfers between devices: 18.4 us -> 5.35 us
    ppermute x8, waiting for transfers between devices: 18.3 us -> 0.5 us  [swap(): return lax.ppermute(value, axis, [(i, i ^ bit) for i in range(size)])]
    ppermute x3, waiting for transfers between devices: 0.01 us -> 4.86 us  [peers(): lax.ppermute(value, axis, [(i, (i + d) % size) for i in range(size)])]
    unnamed x15 -> x17, local copies, waits for them, and re-layouts: 38.4 us -> 37.8 us
  transfers between devices with their start and end apart: 11 -> 11, of which waited for: 6 -> 2; matrix products, arithmetic and copies ran while one was open for 17% -> 19% of each run, Pallas kernels for 12% -> 13%
where the time goes in v1:
time: 155 us
  Pallas kernels  92.1 us (59%)
  local copies, waits for them, and re-layouts  43.4 us (28%)
  starting transfers between devices  11.2 us (7%)
  waiting for transfers between devices  5.35 us (3%)
  other arithmetic  1.84 us (1%)
    pallas_call x1, Pallas kernels, per_device(): pl.pallas_call(functools.partial(main_kernel, step_images=n_b, half=half,...  62.4 us
    unnamed x17, local copies, waits for them, and re-layouts  37.8 us
    pallas_call x4, Pallas kernels, finish(): pl.pallas_call(functools.partial(finish_kernel, step_images=n_c, half=hal...  20.5 us
    pallas_call x1, Pallas kernels, per_device(): pl.pallas_call(functools.partial(stats_kernel, step_images=n_a, half=half...  9.19 us
    ppermute x8, starting transfers between devices, swap(): return lax.ppermute(value, axis, [(i, i ^ bit) for i in range(size)])  7.73 us
    ppermute x3, waiting for transfers between devices, peers(): lax.ppermute(value, axis, [(i, (i + d) % size) for i in range(size)])  4.86 us
    ppermute x3, starting transfers between devices, peers(): lax.ppermute(value, axis, [(i, (i + d) % size) for i in range(size)])  3.42 us
  transfers between devices with their start and end apart: 11, of which 2 were waited for; matrix products, arithmetic and copies ran while one was open for 19% of the time, Pallas kernels for 13%

profile of v1, /device:TPU:0, one launch (start us, length us, event | category | flops | bytes accessed | tf_op | source)
XLA Modules:
  0.0 154.7 jit_solution(7086134994425205632)
XLA Ops:
  0.6 12.9 %copy.40.x_ref.refs_2_.refs_4_ = bf16[48,196,512]{2,1,0:T(8,128)(2,1)} copy(bf16[48,196,512]{2,0,1:T(8,128)(2,1)} %param.7) | data formatting | bytes 19267584 | tf_op args[0]
  13.6 9.2 %row_stats.1.refs_0_ = f32[200,128]{1,0:T(8,128)} custom-call(bf16[48,196,512]{2,1,0:T(8,128)(2,1)} %copy.40.x_ref.refs_2_.refs_4_), custom_call_target="tpu_custom_call" | custom-call | tf_op jit(solution)/shard_map/row_stats/pallas_call | solution.py:176
  22.8 3.0 %collective-permute-start = (f32[200,128]{1,0:T(8,128)}, f32[200,128]{1,0:T(8,128)S(1)}, u32[]{:S(2)}, u32[]{:S(2)}) collective-permute-start(f32[200,128]{1,0:T(8,128)} %row_stats.1.refs_0_), channel_id=1, source_target_pairs={{0,1},{1,0},{2,3},{3,2},{4,5},{5,4},{6,7},{7,6},{8,9},{9,8},{10,11... | collective-permute-start | bytes 307208 | tf_op jit(solution)/shard_map/ppermute | solution.py:147
  26.3 12.9 %copy.47.refs_3_ = bf16[48,196,512]{2,1,0:T(8,128)(2,1)} copy(bf16[48,196,512]{2,0,1:T(8,128)(2,1)} %param.13) | data formatting | bytes 19267584 | tf_op args[6]
  39.4 0.8 pad.13.refs_7_
  40.2 0.7 pad.14.refs_8_
  40.8 0.9 fusion.6.refs_6_
  41.8 0.6 copy-done.4
  42.4 62.4 %mix_backward.1 = (bf16[48,196,512]{2,1,0:T(8,128)(2,1)}, f32[200,128]{1,0:T(8,128)}, f32[200,128]{1,0:T(8,128)}, f32[200,128]{1,0:T(8,128)}, f32[512,512]{1,0:T(8,128)}, /*index=5*/f32[8,512]{1,0:T(8,128)}) custom-call(f32[200,128]{1,0:T(8,128)} %row_stats.1.refs_0_, f32[200,128]{1,0:T(8,128)} %copy-done.4, ...), custom_call_target="tpu_custom_call" | custom-call | tf_op jit(solution)/shard_map/mix_backward/pallas_call | solution.py:198
  104.9 4.9 %collective-permute-done.1.refs_1_ = f32[200,128]{1,0:T(8,128)S(1)} collective-permute-done((f32[200,128]{1,0:T(8,128)}, f32[200,128]{1,0:T(8,128)S(1)}, u32[]{:S(2)}, u32[]{:S(2)}) %collective-permute-start.1) | collective-permute-done | bytes 102432 | tf_op jit(solution)/shard_map/ppermute | solution.py:147
  109.8 1.1 dynamic-slice_bitcast_fusion
  111.0 0.7 slice.18
  112.2 5.2 %finish_0.1.refs_5_ = bf16[48,196,512]{2,1,0:T(8,128)(2,1)} custom-call(f32[200,128]{1,0:T(8,128)} %get-tuple-element.33.refs_0_, f32[200,128]{1,0:T(8,128)} %copy-done, f32[200,128]{1,0:T(8,128)} %get-tuple-element.35.refs_2_, f32[200,128]{1,0:T(8,128)} %get-tuple-element.36.refs_3_, ...), custom_call_target="tpu_custom_call", output_to_operand_aliasing={{}: (5, {})} | custom-call | flops 240844800 | bytes 7225344 | tf_op jit(solution)/shard_map/finish_0/pallas_call | solution.py:243
  117.5 1.6 %collective-permute-start.4 = (f32[4,32,512]{2,1,0:T(8,128)S(1)}, f32[4,32,512]{2,1,0:T(8,128)S(1)}, u32[]{:S(2)}, u32[]{:S(2)}) collective-permute-start(f32[4,32,512]{2,1,0:T(8,128)S(1)} %dynamic-slice_bitcast_fusion.1), channel_id=1, source_target_pairs={{0,4},{2,6},{4,0},{6,2},{8,12},{10,14},{12,8},{14,10},{16,20},{18,... | collective-permute-start | bytes 786440 | tf_op jit(solution)/shard_map/ppermute | solution.py:142
  119.1 0.7 slice_add_fusion
  120.4 5.1 %finish_1.1.refs_5_ = bf16[48,196,512]{2,1,0:T(8,128)(2,1)} custom-call(f32[200,128]{1,0:T(8,128)} %get-tuple-element.33.refs_0_, f32[200,128]{1,0:T(8,128)} %copy-done, f32[200,128]{1,0:T(8,128)} %get-tuple-element.35.refs_2_, f32[200,128]{1,0:T(8,128)} %get-tuple-element.36.refs_3_, ...), custom_call_target="tpu_custom_call", output_to_operand_aliasing={{}: (5, {})} | custom-call | flops 240844800 | bytes 7225344 | tf_op jit(solution)/shard_map/finish_1/pallas_call | solution.py:243
  126.0 1.6 %collective-permute-start.6 = (f32[2,32,512]{2,1,0:T(8,128)S(1)}, f32[2,32,512]{2,1,0:T(8,128)S(1)}, u32[]{:S(2)}, u32[]{:S(2)}) collective-permute-start(f32[2,32,512]{2,1,0:T(8,128)S(1)} %dynamic-slice_bitcast_fusion.2), channel_id=1, source_target_pairs={{0,8},{2,10},{4,12},{6,14},{8,0},{10,2},{12,4},{14,6},{16,24},{18,... | collective-permute-start | bytes 393224 | tf_op jit(solution)/shard_map/ppermute | solution.py:142
  128.1 5.1 %finish_2.1.refs_5_ = bf16[48,196,512]{2,1,0:T(8,128)(2,1)} custom-call(f32[200,128]{1,0:T(8,128)} %get-tuple-element.33.refs_0_, f32[200,128]{1,0:T(8,128)} %copy-done, f32[200,128]{1,0:T(8,128)} %get-tuple-element.35.refs_2_, f32[200,128]{1,0:T(8,128)} %get-tuple-element.36.refs_3_, ...), custom_call_target="tpu_custom_call", output_to_operand_aliasing={{}: (5, {})} | custom-call | flops 240844800 | bytes 7225344 | tf_op jit(solution)/shard_map/finish_2/pallas_call | solution.py:243
  133.2 2.7 %collective-permute-start.8 = (f32[1,32,512]{2,1,0:T(8,128)S(1)}, f32[1,32,512]{2,1,0:T(8,128)S(1)}, u32[]{:S(2)}, u32[]{:S(2)}) collective-permute-start(f32[1,32,512]{2,1,0:T(8,128)S(1)} %constant_dynamic-slice_fusion), channel_id=1, source_target_pairs={{0,16},{2,18},{4,20},{6,22},{8,24},{10,26},{12,28},{14,30},{16,0},... | collective-permute-start | bytes 196616 | tf_op jit(solution)/shard_map/ppermute | solution.py:142
  136.2 5.1 %finish_3.1 = bf16[48,196,512]{2,1,0:T(8,128)(2,1)} custom-call(f32[200,128]{1,0:T(8,128)} %get-tuple-element.33.refs_0_, f32[200,128]{1,0:T(8,128)} %copy-done, f32[200,128]{1,0:T(8,128)} %get-tuple-element.35.refs_2_, f32[200,128]{1,0:T(8,128)} %get-tuple-element.36.refs_3_, ...), custom_call_target="tpu_custom_call", output_to_operand_aliasing={{}: (5, {})} | custom-call | flops 240844800 | bytes 7225344 | tf_op jit(solution)/shard_map/finish_3/pallas_call | solution.py:243
  141.8 0.6 fusion.8
  142.4 11.0 %copy.52 = bf16[48,196,512]{2,0,1:T(8,128)(2,1)} copy(bf16[48,196,512]{2,1,0:T(8,128)(2,1)} %finish_3.1) | data formatting | bytes 19267584
  153.4 0.6 slice_bitcast_fusion
  154.0 0.7 slice_reduce_fusion
  (45 shorter events, 3.7 us)
Async XLA Ops:
  13.6 12.2 %copy-start.5 = (f32[512]{0:T(512)S(1)}, f32[512]{0:T(512)}, u32[]{:S(2)}) copy-start(f32[512]{0:T(512)} %param.11) | copy-start | bytes 6148
  13.6 12.6 %copy-start.2 = (bf16[512,196]{0,1:T(8,128)(2,1)S(1)}, bf16[512,196]{0,1:T(8,128)(2,1)}, u32[]{:S(2)}) copy-start(bf16[512,196]{0,1:T(8,128)(2,1)} %param.10) | copy-start | bytes 602116
  22.8 19.0 %collective-permute-start = (f32[200,128]{1,0:T(8,128)}, f32[200,128]{1,0:T(8,128)S(1)}, u32[]{:S(2)}, u32[]{:S(2)}) collective-permute-start(f32[200,128]{1,0:T(8,128)} %row_stats.1.refs_0_), channel_id=1, source_target_pairs={{0,1},{1,0},{2,3},{3,2},{4,5},{5,4},{6,7},{7,6},{8,9},{9,8},{10,11... | collective-permute-start | bytes 307208 | tf_op jit(solution)/shard_map/ppermute | solution.py:147
  26.3 12.9 %copy-start.3 = (bf16[196,512]{1,0:T(8,128)(2,1)S(1)}, bf16[196,512]{1,0:T(8,128)(2,1)}, u32[]{:S(2)}) copy-start(bf16[196,512]{1,0:T(8,128)(2,1)} %param.12) | copy-start | bytes 602116
  41.8 0.7 copy-start.4
  104.8 4.9 %collective-permute-start.1 = (f32[200,128]{1,0:T(8,128)}, f32[200,128]{1,0:T(8,128)S(1)}, u32[]{:S(2)}, u32[]{:S(2)}) collective-permute-start(f32[200,128]{1,0:T(8,128)} %get-tuple-element.33.refs_0_), channel_id=1, source_target_pairs={{0,1},{1,0},{2,3},{3,2},{4,5},{5,4},{6,7},{7,6},{8,9},{9,8},{10,11... | collective-permute-start | bytes 307208 | tf_op jit(solution)/shard_map/ppermute | solution.py:147
  109.8 2.4 %copy-start = (f32[200,128]{1,0:T(8,128)}, f32[200,128]{1,0:T(8,128)S(1)}, u32[]{:S(2)}) copy-start(f32[200,128]{1,0:T(8,128)S(1)} %collective-permute-done.1.refs_1_) | copy-start | bytes 307204
  110.9 6.5 %collective-permute-start.2 = (f32[8,32,512]{2,1,0:T(8,128)S(1)}, f32[8,32,512]{2,1,0:T(8,128)S(1)}, u32[]{:S(2)}, u32[]{:S(2)}) collective-permute-start(f32[8,32,512]{2,1,0:T(8,128)S(1)} %dynamic-slice_bitcast_fusion), channel_id=1, source_target_pairs={{0,2},{2,0},{4,6},{6,4},{8,10},{10,8},{12,14},{14,12},{16,18},{18,... | collective-permute-start | bytes 1572872 | tf_op jit(solution)/shard_map/ppermute | solution.py:142
  111.7 5.7 %collective-permute-start.3 = (f32[2,512]{1,0:T(2,128)S(1)}, f32[2,512]{1,0:T(2,128)S(1)}, u32[]{:S(2)}, u32[]{:S(2)}) collective-permute-start(f32[2,512]{1,0:T(2,128)S(1)} %slice.18), channel_id=1, source_target_pairs={{0,2},{2,0},{4,6},{6,4},{8,10},{10,8},{12,14},{14,12},{16,18},{18,... | collective-permute-start | bytes 12296 | tf_op jit(solution)/shard_map/ppermute | solution.py:142
  112.2 5.2 %copy-start.1 = (f32[512,512]{1,0:T(8,128)S(1)}, f32[512,512]{1,0:T(8,128)}, u32[]{:S(2)}) copy-start(f32[512,512]{1,0:T(8,128)} %get-tuple-element.31) | copy-start | bytes 3145732
  117.5 8.4 %collective-permute-start.4 = (f32[4,32,512]{2,1,0:T(8,128)S(1)}, f32[4,32,512]{2,1,0:T(8,128)S(1)}, u32[]{:S(2)}, u32[]{:S(2)}) collective-permute-start(f32[4,32,512]{2,1,0:T(8,128)S(1)} %dynamic-slice_bitcast_fusion.1), channel_id=1, source_target_pairs={{0,4},{2,6},{4,0},{6,2},{8,12},{10,14},{12,8},{14,10},{16,20},{18,... | collective-permute-start | bytes 786440 | tf_op jit(solution)/shard_map/ppermute | solution.py:142
  119.9 6.1 %collective-permute-start.5 = (f32[2,512]{1,0:T(2,128)S(1)}, f32[2,512]{1,0:T(2,128)S(1)}, u32[]{:S(2)}, u32[]{:S(2)}) collective-permute-start(f32[2,512]{1,0:T(2,128)S(1)} %slice_add_fusion), channel_id=1, source_target_pairs={{0,4},{2,6},{4,0},{6,2},{8,12},{10,14},{12,8},{14,10},{16,20},{18,... | collective-permute-start | bytes 12296 | tf_op jit(solution)/shard_map/ppermute | solution.py:142
  126.0 7.2 %collective-permute-start.6 = (f32[2,32,512]{2,1,0:T(8,128)S(1)}, f32[2,32,512]{2,1,0:T(8,128)S(1)}, u32[]{:S(2)}, u32[]{:S(2)}) collective-permute-start(f32[2,32,512]{2,1,0:T(8,128)S(1)} %dynamic-slice_bitcast_fusion.2), channel_id=1, source_target_pairs={{0,8},{2,10},{4,12},{6,14},{8,0},{10,2},{12,4},{14,6},{16,24},{18,... | collective-permute-start | bytes 393224 | tf_op jit(solution)/shard_map/ppermute | solution.py:142
  127.6 5.5 %collective-permute-start.7 = (f32[2,512]{1,0:T(2,128)S(1)}, f32[2,512]{1,0:T(2,128)S(1)}, u32[]{:S(2)}, u32[]{:S(2)}) collective-permute-start(f32[2,512]{1,0:T(2,128)S(1)} %add.74), channel_id=1, source_target_pairs={{0,8},{2,10},{4,12},{6,14},{8,0},{10,2},{12,4},{14,6},{16,24},{18,... | collective-permute-start | bytes 12296 | tf_op jit(solution)/shard_map/ppermute | solution.py:142
  133.2 8.1 %collective-permute-start.8 = (f32[1,32,512]{2,1,0:T(8,128)S(1)}, f32[1,32,512]{2,1,0:T(8,128)S(1)}, u32[]{:S(2)}, u32[]{:S(2)}) collective-permute-start(f32[1,32,512]{2,1,0:T(8,128)S(1)} %constant_dynamic-slice_fusion), channel_id=1, source_target_pairs={{0,16},{2,18},{4,20},{6,22},{8,24},{10,26},{12,28},{14,30},{16,0},... | collective-permute-start | bytes 196616 | tf_op jit(solution)/shard_map/ppermute | solution.py:142
  135.9 5.5 %collective-permute-start.9 = (f32[2,512]{1,0:T(2,128)S(1)}, f32[2,512]{1,0:T(2,128)S(1)}, u32[]{:S(2)}, u32[]{:S(2)}) collective-permute-start(f32[2,512]{1,0:T(2,128)S(1)} %add.77), channel_id=1, source_target_pairs={{0,16},{2,18},{4,20},{6,22},{8,24},{10,26},{12,28},{14,30},{16,0},... | collective-permute-start | bytes 12296 | tf_op jit(solution)/shard_map/ppermute | solution.py:142
  141.4 11.9 %collective-permute-start.10 = (f32[32,512]{1,0:T(8,128)S(1)}, f32[32,512]{1,0:T(8,128)S(1)}, u32[]{:S(2)}, u32[]{:S(2)}) collective-permute-start(f32[32,512]{1,0:T(8,128)S(1)} %add_bitcast_fusion), channel_id=1, source_target_pairs={{0,1},{1,0},{2,3},{3,2},{4,5},{5,4},{6,7},{7,6},{8,9},{9,8},{10,11... | collective-permute-start | bytes 196616 | tf_op jit(solution)/shard_map/ppermute | solution.py:147
